TPU v7x, 32 devices: a whole 2x2x4 slice. The times are simulated.
32 devices in a mesh: gx: 16 (over z, y, x), gy: 2 (over core).
Axes of the slice: x: 2, y: 2, z: 4, core: 2. Of those that a mesh axis runs over, the one named last changes fastest.
Arguments:
- droplets: float32 [2, 32, 32, 1024], P(None, None, 'gx', 'gy'), as said below
- moves: int32 [2, 32, 32, 1024], P(None, None, 'gx', 'gy'), may hold values from 0 to 8, as said below
- pairing: int32 [2, 32, 32, 1024], P(None, None, 'gx', 'gy'), may hold values from 0 to 31, as said below
- collisions: int32 [2, 16, 32, 1024], P(None, None, 'gx', 'gy'), may hold values from 0 to 3
Outputs:
- droplets_out: float32 [2, 32, 32, 1024], P(None, None, 'gx', 'gy')
- moments: float32 [2, 2, 16], replicated
Inputs may be any that keep to these rules, and one draw needn't show every extreme that they name: `droplets`: entry 0 holds whole-number multiplicities from 24 to below 300, entry 1 masses from 0.05 to 2. `moves`: A code c means a step of c // 3 - 1 along x and c % 3 - 1 along y. In each step, slot and level, all droplets of one y-row take the same x-step and all droplets landing in one x-column take the same y-step, so every cell and slot receives exactly one droplet. `pairing`: for each step and cell, the entries along the slot dimension are a permutation of 0 to 31.
All inputs are finite; a program needn't handle non-finite values.
Results may differ from a plain program's by a relative error of at most 0.0003.
Values sent between devices are 32-bit elements; how exact they have to be, the bound alone decides.
A program may use at most 64 MiB of HBM per device.

v0:
```python
import jax
import jax.numpy as jnp
from jax import lax
from jax.sharding import PartitionSpec as P

LEVELS = 16


count_unit = 4096.0


def padded(array, sides, width):
    for axis, dim in sides:
        size, length = (lax.axis_size(axis), array.shape[dim])
        up = [(i, (i + 1) % size) for i in range(size)]
        down = [(j, i) for i, j in up]
        last = lax.slice_in_dim(array, length - width, length, axis=dim)
        leading = lax.slice_in_dim(array, 0, width, axis=dim)
        before = lax.ppermute(last, axis, up)
        after = lax.ppermute(leading, axis, down)
        array = jnp.concatenate([before, array, after], axis=dim)
    return array


def spread(state, codes):
    twos, slots, cols, rows, levels = state.shape
    extended = jnp.zeros((twos, slots, cols + 2, rows + 2, levels), state.dtype)
    for direction in range(9):
        step_x = direction // 3 - 1
        step_y = direction % 3 - 1
        chosen = jnp.where((codes == direction)[None], state, jnp.zeros_like(state))
        extended = extended + jnp.pad(
            chosen, ((0, 0), (0, 0), (1 + step_x, 1 - step_x), (1 + step_y, 1 - step_y), (0, 0))
        )
    return extended


def settle(extended, cols, rows):
    twos, slots, wide, tall, levels = extended.shape
    rims = jnp.stack([extended[:, :, 0], extended[:, :, cols + 1]], axis=2).reshape(
        twos, slots, 2, (rows + 2) * levels
    )
    got = padded(rims, (("gx", 2),), 1).reshape(twos, slots, 4, rows + 2, levels)
    middle = (
        extended[:, :, 1 : cols + 1]
        .at[:, :, 0]
        .add(got[:, :, 0])
        .at[:, :, cols - 1]
        .add(got[:, :, 3])
    )
    rims = jnp.stack([middle[:, :, :, 0], middle[:, :, :, rows + 1]], axis=2).reshape(
        twos, slots, 2, cols * levels
    )
    got = padded(rims, (("gy", 2),), 1).reshape(twos, slots, 4, cols, levels)
    block = (
        middle[:, :, :, 1 : rows + 1]
        .at[:, :, :, 0]
        .add(got[:, :, 0])
        .at[:, :, :, rows - 1]
        .add(got[:, :, 3])
    )
    return block


def collide(first_count, second_count, first_mass, second_mass, tries):
    big_first = first_count >= second_count
    larger = jnp.where(big_first, first_count, second_count)
    smaller = jnp.where(big_first, second_count, first_count)
    larger_mass = jnp.where(big_first, first_mass, second_mass)
    smaller_mass = jnp.where(big_first, second_mass, first_mass)
    taken = jnp.minimum(tries, larger // smaller)
    remain = larger - taken * smaller
    splits = remain == 0
    halved = smaller // 2
    larger_new = jnp.where(splits, halved, remain)
    smaller_new = jnp.where(splits, smaller - halved, smaller)
    grown = smaller_mass + taken.astype(first_mass.dtype) * larger_mass
    larger_mass_new = jnp.where(splits, grown, larger_mass)
    first_new = jnp.where(big_first, larger_new, smaller_new)
    second_new = jnp.where(big_first, smaller_new, larger_new)
    first_mass_new = jnp.where(big_first, larger_mass_new, grown)
    second_mass_new = jnp.where(big_first, grown, larger_mass_new)
    return (first_new, second_new, first_mass_new, second_mass_new)


def pair_column(counts_f, masses, order, tries):
    slots = counts_f.shape[0]
    slot_ids = lax.broadcasted_iota(jnp.int32, (slots, slots, 1), 1)
    hits = order[:, None, :] == slot_ids
    counts = counts_f.astype(jnp.int32)
    counts_p = jnp.sum(jnp.where(hits, counts[None], 0), axis=1)
    masses_p = jnp.sum(jnp.where(hits, masses[None], jnp.zeros_like(masses)[None]), axis=1)
    first_new, second_new, first_mass, second_mass = collide(
        counts_p[0::2], counts_p[1::2], masses_p[0::2], masses_p[1::2], tries
    )
    counts_pair = jnp.stack([first_new, second_new], axis=1).reshape(counts_p.shape)
    masses_pair = jnp.stack([first_mass, second_mass], axis=1).reshape(masses_p.shape)
    counts_new = jnp.sum(jnp.where(hits, counts_pair[:, None], 0), axis=0)
    masses_new = jnp.sum(
        jnp.where(hits, masses_pair[:, None], jnp.zeros_like(masses_pair)[:, None]), axis=0
    )
    return (counts_new.astype(counts_f.dtype), masses_new)


def coalesce(block, order, tries):
    twos, slots, cols, rows, levels = block.shape
    flat = block.reshape(twos, slots, cols, rows * levels)
    results = []
    for column in range(cols):
        counts_new, masses_new = pair_column(
            flat[0, :, column], flat[1, :, column], order[:, column], tries[:, column]
        )
        results.append(jnp.stack([counts_new, masses_new]))
    return jnp.stack(results, axis=2).reshape(block.shape)


def shards(droplets, moves, pairing, collisions):
    twos, slots, cols, flat = droplets.shape
    levels = LEVELS
    rows = flat // levels
    state = droplets.reshape(twos, slots, cols, rows, levels)
    totals = []
    for step in range(moves.shape[0]):
        codes = moves[step].reshape(slots, cols, rows, levels)
        state = settle(spread(state, codes), cols, rows)
        state = coalesce(state, pairing[step], collisions[step])
        count_sum = jnp.sum(state[0], axis=(0, 1, 2))
        liquid_sum = jnp.sum(state[0] * state[1], axis=(0, 1, 2))
        terms = jnp.stack([count_sum, liquid_sum])
        totals.append(lax.psum(terms, ("gx", "gy")))
    summed = jnp.stack(totals)
    cells_x = cols * lax.axis_size("gx")
    cells_y = rows * lax.axis_size("gy")
    moments = summed / (cells_x * cells_y * count_unit)
    return (state.reshape(droplets.shape), moments)


def solution(mesh):
    placed = (
        P(None, None, "gx", "gy"),
        P(None, None, "gx", "gy"),
        P(None, None, "gx", "gy"),
        P(None, None, "gx", "gy"),
    )
    return jax.shard_map(
        shards,
        mesh=mesh,
        in_specs=placed,
        out_specs=(P(None, None, "gx", "gy"), P()),
        check_vma=False,
    )
```

profile of v0, /device:TPU:0, one launch (start us, length us, event | category | flops | bytes accessed | tf_op | source)
XLA Modules:
  0.0 107.8 jit_solution(15676673924151060772)
XLA Ops:
  0.6 1.0 fusion.55
  1.9 0.8 broadcast_compare_fusion.16
  3.1 1.2 %broadcast_select_fusion.17 = (f32[2,32,2,32,16]{1,4,3,2,0:T(8,128)S(1)}, f32[2,32,2,32,16]{1,4,3,2,0:T(8,128)S(1)}, f32[2,32,2,32,16]{1,4,3,2,0:T(8,128)S(1)}, ...) fusion(f32[2,32,2,32,16]{1,4,3,2,0:T(8,128)S(1)} %bitcast.219, ...), kind=kLoop, calls=%fused_computation.50 | loop fusion | flops 589824 | bytes 2916352 | tf_op jit(solution)/shard_map/jit(_where)/select_n | solution.py:31
  5.2 1.1 %copy.85 = f32[2,32,1,544]{3,1,2,0:T(8,128)} copy(f32[2,32,1,544]{1,3,2,0:T(8,128)S(1)} %get-tuple-element.121) | data formatting | bytes 278528 | tf_op jit(solution)/shard_map/slice | solution.py:17
  6.3 3.0 %collective-permute-start = (f32[2,32,1,544]{3,1,2,0:T(8,128)}, f32[2,32,1,544]{3,1,2,0:T(8,128)}, u32[]{:S(2)}, u32[]{:S(2)}) collective-permute-start(f32[2,32,1,544]{3,1,2,0:T(8,128)} %copy.85), channel_id=1, source_target_pairs={{0,2},{2,4},{4,6},{6,8},{8,10},{10,12},{12,14},{14,16},{16,18},{18... | collective-permute-start | bytes 417800 | tf_op jit(solution)/shard_map/ppermute | solution.py:19
  9.2 0.9 copy.88
  10.1 4.0 %collective-permute-start.1 = (f32[2,32,1,544]{3,1,2,0:T(8,128)}, f32[2,32,1,544]{3,1,2,0:T(8,128)}, u32[]{:S(2)}, u32[]{:S(2)}) collective-permute-start(f32[2,32,1,544]{3,1,2,0:T(8,128)} %copy.88), channel_id=1, source_target_pairs={{2,0},{4,2},{6,4},{8,6},{10,8},{12,10},{14,12},{16,14},{18,16},{20... | collective-permute-start | bytes 417800 | tf_op jit(solution)/shard_map/ppermute | solution.py:20
  14.8 1.0 copy.130
  15.9 2.5 %broadcast_compare_fusion.17 = (pred[1,32,2,512]{1,3,2,0:T(8,128)(4,1)}, pred[1,32,2,512]{1,3,2,0:T(8,128)(4,1)}, pred[1,32,2,512]{1,3,2,0:T(8,128)(4,1)}, pred[...) fusion(s32[1,32,2,512]{1,3,2,0:T(8,128)} %copy.130), kind=kLoop, calls=%fused_computation.87 | loop fusion | flops 294912 | bytes 425984 | tf_op jit(solution)/shard_map/eq | solution.py:31
  18.4 2.0 %fusion.56 = (s32[32,1,512]{2,1,0:T(1,128)}, s32[32,1,512]{2,1,0:T(1,128)}, s32[32,1,512]{2,1,0:T(1,128)}, s32[32,1,512]{2,1,0:T(1,128)}) fusion(s32[32,2,512]{2,1,0:T(2,128)} %get-tuple-element.166, s32[32,2,512]{2,1,0:T(2,128)} %get-tuple-element.167), kind=kLoop, calls=%fused_computation.232 | loop fusion | bytes 524288 | tf_op jit(solution)/shard_map/slice | solution.py:111
  20.4 0.9 fusion.57
  21.3 1.9 %copy.86 = f32[2,32,1,544]{1,3,0,2:T(8,128)} copy(f32[2,32,1,544]{3,1,2,0:T(8,128)} %collective-permute-done) | data formatting | bytes 278528 | tf_op jit(solution)/shard_map/ppermute | solution.py:19
  23.3 1.1 %fusion.3 = f32[2,32,2,34,16]{1,4,3,2,0:T(8,128)S(1)} fusion(f32[2,32,2,34,16]{1,4,3,2,0:T(8,128)S(1)} %slice-done, f32[2,32,1,34,16]{1,4,3,2,0:T(8,128)} %bitcast.220, f32[2,32,4,34,16]{1,4,3,2,0:T(8,128)S(1)} %copy-done.1), kind=kLoop, calls=%fused_computation.32 | loop fusion | flops 34816 | bytes 1253376 | tf_op jit(solution)/shard_map/scatter-add | solution.py:47
  24.4 1.2 %copy.89 = f32[2,32,1,544]{1,3,0,2:T(8,128)S(1)} copy(f32[2,32,1,544]{3,1,2,0:T(8,128)} %collective-permute-done.1) | data formatting | bytes 278528 | tf_op jit(solution)/shard_map/ppermute | solution.py:20
  29.9 0.8 select_bitcast_fusion.7
  31.8 0.7 fusion.15
  38.5 0.9 fusion.52
  39.3 0.9 copy.106
  40.3 0.9 maximum_bitcast_fusion.3
  41.8 0.8 reduce_sum.225
  42.6 1.4 %reduce_sum.228 = f32[32,16]{1,0:T(8,128)} reshape(f32[512]{0:T(512)} %get-tuple-element.105) | data formatting | bytes 4096 | tf_op jit(solution)/shard_map/reduce_sum | solution.py:128
  44.5 0.7 reduce_sum.229
  45.2 1.9 %copy.109 = f32[2,32,1,544]{3,1,2,0:T(8,128)} copy(f32[2,32,1,544]{1,3,2,0:T(8,128)} %get-tuple-element.116) | data formatting | bytes 278528 | tf_op jit(solution)/shard_map/slice | solution.py:18
  47.1 5.6 %collective-permute-start.5 = (f32[2,32,1,544]{3,1,2,0:T(8,128)}, f32[2,32,1,544]{3,1,2,0:T(8,128)}, u32[]{:S(2)}, u32[]{:S(2)}) collective-permute-start(f32[2,32,1,544]{3,1,2,0:T(8,128)} %copy.109), channel_id=1, source_target_pairs={{2,0},{4,2},{6,4},{8,6},{10,8},{12,10},{14,12},{16,14},{18,16},{20... | collective-permute-start | bytes 417800 | tf_op jit(solution)/shard_map/ppermute | solution.py:20
  52.7 1.9 %copy.107 = f32[2,32,1,544]{1,3,0,2:T(8,128)} copy(f32[2,32,1,544]{3,1,2,0:T(8,128)} %collective-permute-done.4) | data formatting | bytes 278528 | tf_op jit(solution)/shard_map/ppermute | solution.py:19
  54.6 1.1 %fusion.1 = f32[2,32,2,34,16]{1,4,3,2,0:T(8,128)S(1)} fusion(f32[2,32,2,34,16]{1,4,3,2,0:T(8,128)S(1)} %slice.539, f32[2,32,1,34,16]{1,4,3,2,0:T(8,128)} %bitcast.221, f32[2,32,4,34,16]{1,4,3,2,0:T(8,128)S(1)} %pad_add_fusion), kind=kLoop, calls=%fused_computation.28 | loop fusion | flops 34816 | bytes 1253376 | tf_op jit(solution)/shard_map/scatter-add | solution.py:47
  55.8 1.0 collective-permute-done.5
  56.7 1.1 %copy.110 = f32[2,32,1,544]{1,3,0,2:T(8,128)S(1)} copy(f32[2,32,1,544]{3,1,2,0:T(8,128)} %collective-permute-done.5) | data formatting | bytes 278528 | tf_op jit(solution)/shard_map/ppermute | solution.py:20
  62.0 0.8 select_bitcast_fusion.3
  63.3 0.7 fusion.19
  65.8 0.9 copy.125
  66.8 40.4 %all-reduce.18 = (f32[1,2,16]{2,1,0:T(2,128)S(1)}, f32[1,2,16]{2,1,0:T(2,128)S(1)}) all-reduce(f32[1,2,16]{2,1,0:T(2,128)S(1)} %maximum_bitcast_fusion.5, f32[1,2,16]{2,1,0:T(2,128)S(1)} %maximum_bitcast_fusion.4), channel_id=1, replica_groups=mesh['gx'=16,'gy'=2] {'gx','gy'}, use_global_device_ids=true, to_apply=%region_25.26 | all-reduce | flops 64 | bytes 512 | tf_op jit(solution)/shard_map/psum | solution.py:130
  (171 shorter events, 21.2 us)
Async XLA Ops:
  0.6 2.1 %copy-start.12 = (f32[2,32,2,512]{3,2,1,0:T(2,128)S(1)}, f32[2,32,2,512]{3,2,1,0:T(2,128)}, u32[]{:S(2)}) copy-start(f32[2,32,2,512]{3,2,1,0:T(2,128)} %param.20) | copy-start | bytes 786436
  4.9 9.2 %copy-start = (f32[2,32,4,34,16]{1,4,3,2,0:T(8,128)}, f32[2,32,4,34,16]{1,4,3,2,0:T(8,128)S(1)}, u32[]{:S(2)}) copy-start(f32[2,32,4,34,16]{1,4,3,2,0:T(8,128)S(1)} %pad_add_fusion.1) | copy-start | bytes 1671172
  6.3 15.0 %collective-permute-start = (f32[2,32,1,544]{3,1,2,0:T(8,128)}, f32[2,32,1,544]{3,1,2,0:T(8,128)}, u32[]{:S(2)}, u32[]{:S(2)}) collective-permute-start(f32[2,32,1,544]{3,1,2,0:T(8,128)} %copy.85), channel_id=1, source_target_pairs={{0,2},{2,4},{4,6},{6,8},{8,10},{10,12},{12,14},{14,16},{16,18},{18... | collective-permute-start | bytes 417800 | tf_op jit(solution)/shard_map/ppermute | solution.py:19
  10.1 4.0 %copy-start.13 = (s32[2,32,2,512]{3,2,1,0:T(2,128)S(1)}, s32[2,32,2,512]{3,2,1,0:T(2,128)}, u32[]{:S(2)}) copy-start(s32[2,32,2,512]{3,2,1,0:T(2,128)} %param.22) | copy-start | bytes 786436
  10.1 14.3 %collective-permute-start.1 = (f32[2,32,1,544]{3,1,2,0:T(8,128)}, f32[2,32,1,544]{3,1,2,0:T(8,128)}, u32[]{:S(2)}, u32[]{:S(2)}) collective-permute-start(f32[2,32,1,544]{3,1,2,0:T(8,128)} %copy.88), channel_id=1, source_target_pairs={{2,0},{4,2},{6,4},{8,6},{10,8},{12,10},{14,12},{16,14},{18,16},{20... | collective-permute-start | bytes 417800 | tf_op jit(solution)/shard_map/ppermute | solution.py:20
  14.1 9.1 %copy-start.1 = (f32[2,32,4,34,16]{1,4,3,2,0:T(8,128)S(1)}, f32[2,32,4,34,16]{1,4,3,2,0:T(8,128)}, u32[]{:S(2)}) copy-start(f32[2,32,4,34,16]{1,4,3,2,0:T(8,128)} %copy-done) | copy-start | bytes 1671172
  14.1 9.1 %slice-start = ((f32[2,32,4,34,16]{1,4,3,2,0:T(8,128)}), f32[2,32,2,34,16]{1,4,3,2,0:T(8,128)S(1)}, s32[]{:S(2)}) async-start(f32[2,32,4,34,16]{1,4,3,2,0:T(8,128)} %copy-done), calls=%async_computation | async-start | bytes 2228224 | tf_op jit(solution)/shard_map/slice | solution.py:45
  24.4 1.5 %copy-start.18 = (s32[32,1,512]{2,1,0:T(1,128)S(1)}, s32[32,1,512]{2,1,0:T(1,128)}, u32[]{:S(2)}) copy-start(s32[32,1,512]{2,1,0:T(1,128)} %get-tuple-element.204) | copy-start | bytes 196612
  24.4 1.5 %copy-start.17 = (s32[32,1,512]{2,1,0:T(1,128)S(1)}, s32[32,1,512]{2,1,0:T(1,128)}, u32[]{:S(2)}) copy-start(s32[32,1,512]{2,1,0:T(1,128)} %get-tuple-element.205) | copy-start | bytes 196612
  24.4 1.5 %copy-start.16 = (s32[32,1,512]{2,1,0:T(1,128)S(1)}, s32[32,1,512]{2,1,0:T(1,128)}, u32[]{:S(2)}) copy-start(s32[32,1,512]{2,1,0:T(1,128)} %get-tuple-element.181) | copy-start | bytes 196612
  24.4 1.6 %copy-start.15 = (s32[32,1,512]{2,1,0:T(1,128)S(1)}, s32[32,1,512]{2,1,0:T(1,128)}, u32[]{:S(2)}) copy-start(s32[32,1,512]{2,1,0:T(1,128)} %get-tuple-element.180) | copy-start | bytes 196612
  25.8 1.3 %collective-permute-start.2 = (f32[2,32,1,32]{1,3,0,2:T(8,128)S(1)}, f32[2,32,1,32]{1,3,0,2:T(8,128)S(1)}, u32[]{:S(2)}, u32[]{:S(2)}) collective-permute-start(f32[2,32,1,32]{1,3,0,2:T(8,128)S(1)} %bitcast.267), channel_id=1, source_target_pairs={{0,1},{1,0},{2,3},{3,2},{4,5},{5,4},{6,7},{7,6},{8,9},{9,8},{10,11... | collective-permute-start | bytes 24584 | tf_op jit(solution)/shard_map/ppermute | solution.py:19
  26.1 1.4 %collective-permute-start.3 = (f32[2,32,1,32]{1,3,0,2:T(8,128)S(1)}, f32[2,32,1,32]{1,3,0,2:T(8,128)S(1)}, u32[]{:S(2)}, u32[]{:S(2)}) collective-permute-start(f32[2,32,1,32]{1,3,0,2:T(8,128)S(1)} %bitcast.266), channel_id=1, source_target_pairs={{1,0},{0,1},{3,2},{2,3},{5,4},{4,5},{7,6},{6,7},{9,8},{8,9},{11,10... | collective-permute-start | bytes 24584 | tf_op jit(solution)/shard_map/ppermute | solution.py:20
  30.8 4.4 %copy-start.9 = (pred[1,32,2,512]{1,3,2,0:T(8,128)(4,1)S(1)}, pred[1,32,2,512]{1,3,2,0:T(8,128)(4,1)}, u32[]{:S(2)}) copy-start(pred[1,32,2,512]{1,3,2,0:T(8,128)(4,1)} %get-tuple-element.148) | copy-start | bytes 98308
  30.8 4.4 %copy-start.10 = (pred[1,32,2,512]{1,3,2,0:T(8,128)(4,1)S(1)}, pred[1,32,2,512]{1,3,2,0:T(8,128)(4,1)}, u32[]{:S(2)}) copy-start(pred[1,32,2,512]{1,3,2,0:T(8,128)(4,1)} %get-tuple-element.155) | copy-start | bytes 98308
  30.8 4.4 %copy-start.11 = (pred[1,32,2,512]{1,3,2,0:T(8,128)(4,1)S(1)}, pred[1,32,2,512]{1,3,2,0:T(8,128)(4,1)}, u32[]{:S(2)}) copy-start(pred[1,32,2,512]{1,3,2,0:T(8,128)(4,1)} %get-tuple-element.156) | copy-start | bytes 98308
  34.6 1.0 copy-start.2
  35.2 0.9 copy-start.6
  35.2 1.0 copy-start.7
  35.2 1.0 copy-start.8
  36.2 0.9 copy-start.3
  36.3 1.0 copy-start.4
  36.3 1.0 copy-start.5
  38.4 1.9 %copy-start.14 = (f32[1,32,512]{2,1,0:T(8,128)S(1)}, f32[1,32,512]{2,1,0:T(8,128)}, u32[]{:S(2)}) copy-start(f32[1,32,512]{2,1,0:T(8,128)} %get-tuple-element.192) | copy-start | bytes 196612
  40.2 12.5 %collective-permute-start.4 = (f32[2,32,1,544]{3,1,2,0:T(8,128)}, f32[2,32,1,544]{3,1,2,0:T(8,128)}, u32[]{:S(2)}, u32[]{:S(2)}) collective-permute-start(f32[2,32,1,544]{3,1,2,0:T(8,128)} %copy.106), channel_id=1, source_target_pairs={{0,2},{2,4},{4,6},{6,8},{8,10},{10,12},{12,14},{14,16},{16,18},{18... | collective-permute-start | bytes 417800 | tf_op jit(solution)/shard_map/ppermute | solution.py:19
  47.1 9.6 %collective-permute-start.5 = (f32[2,32,1,544]{3,1,2,0:T(8,128)}, f32[2,32,1,544]{3,1,2,0:T(8,128)}, u32[]{:S(2)}, u32[]{:S(2)}) collective-permute-start(f32[2,32,1,544]{3,1,2,0:T(8,128)} %copy.109), channel_id=1, source_target_pairs={{2,0},{4,2},{6,4},{8,6},{10,8},{12,10},{14,12},{16,14},{18,16},{20... | collective-permute-start | bytes 417800 | tf_op jit(solution)/shard_map/ppermute | solution.py:20
  54.6 3.5 %copy-start.19 = (f32[16]{0:T(128)S(1)}, f32[16]{0:T(128)}, u32[]{:S(2)}) copy-start(f32[16]{0:T(128)} %reduce_sum.226) | copy-start | bytes 196
  58.0 1.3 %collective-permute-start.6 = (f32[2,32,1,32]{1,3,0,2:T(8,128)S(1)}, f32[2,32,1,32]{1,3,0,2:T(8,128)S(1)}, u32[]{:S(2)}, u32[]{:S(2)}) collective-permute-start(f32[2,32,1,32]{1,3,0,2:T(8,128)S(1)} %bitcast.269), channel_id=1, source_target_pairs={{0,1},{1,0},{2,3},{3,2},{4,5},{5,4},{6,7},{7,6},{8,9},{9,8},{10,11... | collective-permute-start | bytes 24584 | tf_op jit(solution)/shard_map/ppermute | solution.py:19
  58.2 1.4 %collective-permute-start.7 = (f32[2,32,1,32]{1,3,0,2:T(8,128)S(1)}, f32[2,32,1,32]{1,3,0,2:T(8,128)S(1)}, u32[]{:S(2)}, u32[]{:S(2)}) collective-permute-start(f32[2,32,1,32]{1,3,0,2:T(8,128)S(1)} %bitcast.268), channel_id=1, source_target_pairs={{1,0},{0,1},{3,2},{2,3},{5,4},{4,5},{7,6},{6,7},{9,8},{8,9},{11,10... | collective-permute-start | bytes 24584 | tf_op jit(solution)/shard_map/ppermute | solution.py:20
where the time goes:
time: 108 us
  blocking collectives  40.4 us (37%)
  local copies, waits for them, and re-layouts  25.6 us (24%)
  other arithmetic  23.8 us (22%)
  starting transfers between devices  13.8 us (13%)
  waiting for transfers between devices  2.67 us (2%)
  between operations  1.49 us (1%)
    psum x1, blocking collectives, shards(): totals.append(lax.psum(terms, ('gx', 'gy')))  40.4 us
    ppermute x4, starting transfers between devices, padded(): after = lax.ppermute(leading, axis, down)  10.7 us
    unnamed x48, local copies, waits for them, and re-layouts  3.88 us
    ppermute x2, local copies, waits for them, and re-layouts, padded(): before = lax.ppermute(last, axis, up)  3.87 us
    slice x4, local copies, waits for them, and re-layouts, padded(): leading = lax.slice_in_dim(array, 0, width, axis=dim)  3.72 us
    eq x2, other arithmetic, spread(): chosen = jnp.where((codes == direction)[None], state, jnp.zeros_like(state))  3.36 us
    ppermute x4, starting transfers between devices, padded(): before = lax.ppermute(last, axis, up)  3.11 us
    scatter-add x4, other arithmetic, settle(): middle = extended[:, :, 1:cols + 1].at[:, :, 0].add(got[:, :, 0]).at[:, :...  2.53 us
  transfers between devices with their start and end apart: 8, of which 5 were waited for; matrix products, arithmetic and copies ran while one was open for 20% of the time, Pallas kernels for 0%

commit v1 on v0

v1 whole, which is shorter than its diff:
```python
import functools

import jax
import jax.numpy as jnp
from jax import lax
from jax.experimental import pallas as pl
from jax.experimental.pallas import tpu as pltpu
from jax.sharding import PartitionSpec as P

LEVELS = 16
LANES = 128
ROWS = 8
CHUNKS = 4
count_unit = 4096.0
MESH = pl.DeviceIdType.MESH


def roll(value, shift, axis):
    shift = shift % value.shape[axis]
    return value if shift == 0 else pltpu.roll(value, shift, axis)


def tree(values, bits):
    level = 0
    while len(values) > 1:
        values = [
            jnp.where(bits[level], values[i + 1], values[i]) for i in range(0, len(values), 2)
        ]
        level += 1
    return values[0]


def collide(na, nb, ma, mb, tries):
    first = na >= nb
    big, small = jnp.maximum(na, nb), jnp.minimum(na, nb)
    big_m, small_m = jnp.where(first, ma, mb), jnp.where(first, mb, ma)
    most = jnp.where(3.0 * small <= big, 3.0, jnp.where(2.0 * small <= big, 2.0, 1.0))
    taken = jnp.minimum(tries.astype(jnp.float32), most)
    remain = big - taken * small
    split = remain == 0.0
    half = jnp.floor(small * 0.5)
    big_new = jnp.where(split, half, remain)
    small_new = jnp.where(split, small - half, small)
    grown = small_m + taken * big_m
    big_m_new = jnp.where(split, grown, big_m)
    return (
        jnp.where(first, big_new, small_new),
        jnp.where(first, small_new, big_new),
        jnp.where(first, big_m_new, grown),
        jnp.where(first, grown, big_m_new),
    )


def kernel(
    nx, ny, slots, steps, scale,
    drops_hbm, moves_hbm, order_hbm, tries_hbm, out_hbm, mom_ref,
    cur, moves, order, tries, moved, paired, cy_ref,
    send_l, send_r, halo_l, halo_r,
    code_send, code_l, code_r,
    edge_send, edge_dn, edge_up,
    part_y, got_y, part_x, got_x,
    in_sem, out_sem, xs_sem, xl_sem, xr_sem, cs_sem, cl_sem, cr_sem,
    es_sem, ed_sem, eu_sem, ys_sem, yr_sem, gs_sem, gr_sem,
):
    gx, gy = lax.axis_index("gx"), lax.axis_index("gy")
    left, right = (lax.rem(gx + nx - 1, nx), gy), (lax.rem(gx + 1, nx), gy)
    down, up = (gx, lax.rem(gy + ny - 1, ny)), (gx, lax.rem(gy + 1, ny))
    half = slots // 2
    per = half // CHUNKS

    loads = [
        pltpu.make_async_copy(src, dst, in_sem.at[i])
        for i, (src, dst) in enumerate(
            [(drops_hbm, cur.at[0]), (moves_hbm, moves), (order_hbm, order), (tries_hbm, tries)]
        )
    ]
    for load in loads:
        load.start()

    barrier = pltpu.get_barrier_semaphore()
    for d in range(1, nx):
        pl.semaphore_signal(barrier, inc=1, device_id=(lax.rem(gx + d, nx), gy), device_id_type=MESH)
    for d in range(1, ny):
        pl.semaphore_signal(barrier, inc=1, device_id=(gx, lax.rem(gy + d, ny)), device_id_type=MESH)

    row = lax.broadcasted_iota(jnp.int32, (ROWS, LANES), 0)
    lane = lax.broadcasted_iota(jnp.int32, (ROWS, LANES), 1)
    even = lax.rem(row, 2) == 0
    group = lane // LEVELS
    groups = LANES // LEVELS

    def remote(src, dst, ss, rs, dev):
        return pltpu.make_async_remote_copy(
            src_ref=src, dst_ref=dst, send_sem=ss, recv_sem=rs, device_id=dev, device_id_type=MESH
        )

    def chunk_slots(q):
        return [q * per + t for t in range(per)] + [half + q * per + t for t in range(per)]

    def pack_chunk(step, q):
        for v in range(2):
            for t in range(per):
                a, b = cur[step, v, q * per + t], cur[step, v, half + q * per + t]
                send_r[step, q, v, t] = jnp.where(even, roll(a, -1, 0), b)
                send_l[step, q, v, t] = jnp.where(even, a, roll(b, 1, 0))

    def x_copies(step, q):
        return [
            remote(send_r.at[step, q], halo_l.at[step, q], xs_sem.at[step, 0, q], xl_sem.at[step, q], right),
            remote(send_l.at[step, q], halo_r.at[step, q], xs_sem.at[step, 1, q], xr_sem.at[step, q], left),
        ]

    def send_state(step):
        for q in range(CHUNKS):
            pack_chunk(step, q)
        copies = []
        for q in range(CHUNKS):
            pair = x_copies(step, q)
            for c in pair:
                c.start()
            copies.append(pair)
        return copies

    loads[0].wait()
    for q in range(CHUNKS):
        pack_chunk(0, q)
    loads[1].wait()
    for step in range(steps):
        packed = jnp.zeros((ROWS, LANES), jnp.int32)
        for q in range(CHUNKS):
            part = jnp.zeros((ROWS, LANES), jnp.int32)
            for g, s in enumerate(chunk_slots(q)):
                part = jnp.where(group == g, roll(moves[step, s], LEVELS * g, 1), part)
            packed = jnp.where(row // 2 == q, roll(part, 2 * q, 0), packed)
        code_send[step] = packed
    pl.semaphore_wait(barrier, nx + ny - 2)
    code_copies = [
        remote(code_send, code_l, cs_sem.at[0], cl_sem, right),
        remote(code_send, code_r, cs_sem.at[1], cr_sem, left),
    ]
    for c in code_copies:
        c.start()
    copies = []
    for q in range(CHUNKS):
        pair = x_copies(0, q)
        for c in pair:
            c.start()
        copies.append(pair)

    for c in code_copies:
        c.wait()
    for step in range(steps):
        own = code_send[step]
        swapped = jnp.where(even, roll(own, -1, 0), roll(own, 1, 0))
        outer = jnp.where(even, roll(code_l[step], -1, 0), roll(code_r[step], 1, 0))
        from_halo = jnp.where(even, own, 8 - own) >= 6
        landed = jnp.where((own >= 3) & (own < 6), own, jnp.where(from_halo, outer, swapped))
        y_step = lax.rem(landed, 3) - 1
        for q in range(CHUNKS):
            lift = roll(y_step, -2 * q, 0)
            lift = jnp.where(row < 2, lift, 0)
            lift = lift + roll(lift, 2, 0)
            lift = lift + roll(lift, 4, 0)
            for g, s in enumerate(chunk_slots(q)):
                one = jnp.where(group == 0, roll(lift, -LEVELS * g, 1), 0)
                width = LEVELS
                while width < LANES:
                    one = one + roll(one, width, 1)
                    width *= 2
                cy_ref[step, s] = one

    row_totals = []
    loads[2].wait()
    loads[3].wait()
    for step in range(steps):
        edge_copies = []
        for q in range(CHUNKS):
            for c in copies[q]:
                c.wait()
            members = chunk_slots(q)
            for v in range(2):
                packed = jnp.zeros((ROWS, LANES), jnp.float32)
                for g, s in enumerate(members):
                    t = g % per
                    hl, hr = halo_l[step, q, v, t], halo_r[step, q, v, t]
                    if g < per:
                        outer = jnp.where(even, hl, roll(hr, 1, 0))
                    else:
                        outer = jnp.where(even, roll(hl, -1, 0), hr)
                    mine, code = cur[step, v, s], moves[step, s]
                    swapped = jnp.where(even, roll(mine, -1, 0), roll(mine, 1, 0))
                    from_halo = jnp.where(even, code, 8 - code) >= 6
                    new = jnp.where(
                        (code >= 3) & (code < 6), mine, jnp.where(from_halo, outer, swapped)
                    )
                    moved[v, s] = new
                    edges = jnp.where(row < 2, new, roll(new, LEVELS, 1))
                    packed = jnp.where(group == g, roll(edges, LEVELS * g, 1), packed)
                edge_send[step, q, v] = packed
            sends = [remote(edge_send.at[step, q], edge_dn.at[step, q], es_sem.at[step, 0, q], ed_sem.at[step, q], up)]
            if ny > 2:
                sends.append(
                    remote(edge_send.at[step, q], edge_up.at[step, q], es_sem.at[step, 1, q], eu_sem.at[step, q], down)
                )
            for c in sends:
                c.start()
            edge_copies.append(sends)
        for q in range(CHUNKS):
            for c in edge_copies[q]:
                c.wait()
            above = edge_up if ny > 2 else edge_dn
            for v in range(2):
                low, high = edge_dn[step, q, v], above[step, q, v]
                for g, s in enumerate(chunk_slots(q)):
                    mine, dy = moved[v, s], cy_ref[step, s]
                    fwd, bwd = roll(mine, LEVELS, 1), roll(mine, -LEVELS, 1)
                    fwd_in = roll(jnp.where(row >= ROWS - 2, roll(low, -LEVELS * g, 1), fwd), 2, 0)
                    bwd_in = roll(jnp.where(row < 2, roll(high, -LEVELS * (g + 1), 1), bwd), -2, 0)
                    fwd = jnp.where(group == 0, fwd_in, fwd)
                    bwd = jnp.where(group == groups - 1, bwd_in, bwd)
                    moved[v, s] = jnp.where(dy == 0, mine, jnp.where(dy > 0, fwd, bwd))

        def pair_body(i, _):
            found = []
            for k in range(2):
                index = order[step, 2 * i + k]
                bits = [(index & (1 << b)) != 0 for b in range((slots - 1).bit_length())]
                for v in range(2):
                    found.append(tree([moved[v, s] for s in range(slots)], bits))
            na, ma, nb, mb = found
            na, nb, ma, mb = collide(na, nb, ma, mb, tries[step, i])
            paired[0, 2 * i] = na
            paired[0, 2 * i + 1] = nb
            paired[1, 2 * i] = ma
            paired[1, 2 * i + 1] = mb
            return 0

        lax.fori_loop(0, half, pair_body, 0)

        width = 8

        def slot_body(i, sums):
            base = i * width
            counts = [jnp.zeros((ROWS, LANES), jnp.float32)] * width
            masses = [jnp.zeros((ROWS, LANES), jnp.float32)] * width
            for p in range(slots):
                index = order[step, p] - base
                pn, pm = paired[0, p], paired[1, p]
                for k in range(width):
                    hit = index == k
                    counts[k] = jnp.where(hit, pn, counts[k])
                    masses[k] = jnp.where(hit, pm, masses[k])
            count, liquid = sums
            for k in range(width):
                cur[step + 1, 0, base + k] = counts[k]
                cur[step + 1, 1, base + k] = masses[k]
                count = count + counts[k]
                liquid = liquid + counts[k] * masses[k]
            return count, liquid

        zero = jnp.zeros((ROWS, LANES), jnp.float32)
        sums = lax.fori_loop(0, slots // width, slot_body, (zero, zero))
        if step + 1 < steps:
            copies = send_state(step + 1)
        for total in sums:
            shift = ROWS // 2
            while shift:
                total = total + roll(total, shift, 0)
                shift //= 2
            shift = LANES // 2
            while shift >= LEVELS:
                total = total + roll(total, shift, 1)
                shift //= 2
            row_totals.append(total)

    result = pltpu.make_async_copy(cur.at[steps], out_hbm, out_sem)
    result.start()

    mine = row_totals[0]
    for i in range(1, len(row_totals)):
        mine = jnp.where(group == i, row_totals[i], mine)

    def gather_sum(value, part, got, ss, rs, me, size, peer):
        part[...] = value
        sends = [
            remote(part, got.at[d - 1], ss.at[d - 1], rs.at[d - 1], peer(lax.rem(me + d, size)))
            for d in range(1, size)
        ]
        for c in sends:
            c.start()
        for c in sends:
            c.wait()
        total = jnp.zeros_like(value)
        for i in range(size):
            term = jnp.where(me == i, 1.0, 0.0) * value
            for d in range(1, size):
                term = term + jnp.where(lax.rem(me + size - d, size) == i, 1.0, 0.0) * got[d - 1]
            total = total + term
        return total

    mine = gather_sum(mine, part_y, got_y, ys_sem, yr_sem, gy, ny, lambda p: (gx, p))
    part_x[...] = mine
    sends = []
    for d in range(1, nx):
        c = remote(part_x, got_x.at[gx], gs_sem.at[d - 1], gr_sem.at[d - 1], (lax.rem(gx + d, nx), gy))
        c.start()
        sends.append(c)
    got_x[gx] = mine
    for c in sends:
        c.wait()
    total = got_x[0]
    for i in range(1, nx):
        total = total + got_x[i]
    total = total * scale
    for i in range(steps):
        for v in range(2):
            mom_ref[i, v : v + 1, :] = roll(total, -LEVELS * (2 * i + v), 1)[0:1, :LEVELS]
    result.wait()


def solution(mesh):
    nx, ny = mesh.shape["gx"], mesh.shape["gy"]

    def body(droplets, moves, pairing, collisions):
        two, slots, cols, flat = droplets.shape
        steps, tiles = moves.shape[0], flat // LANES
        assert cols * tiles == ROWS and cols == 2

        def view(a):
            lead = a.shape[:2]
            return a.reshape(*lead, cols, tiles, LANES).swapaxes(2, 3).reshape(*lead, ROWS, LANES)

        f32, i32 = jnp.float32, jnp.int32
        tile = (ROWS, LANES)
        per = slots // 2 // CHUNKS
        dma = pltpu.SemaphoreType.DMA
        halo = pltpu.VMEM((steps, CHUNKS, 2, per, *tile), f32)
        edge = pltpu.VMEM((steps, CHUNKS, 2, *tile), f32)
        code = pltpu.VMEM((steps, *tile), i32)
        scale = 1.0 / (cols * nx * (flat // LEVELS) * ny * count_unit)
        any_space = pl.BlockSpec(memory_space=pl.ANY)
        out, moments = pl.pallas_call(
            functools.partial(kernel, nx, ny, slots, steps, scale),
            out_shape=(
                jax.ShapeDtypeStruct((two, slots, *tile), f32),
                jax.ShapeDtypeStruct((steps, 2, LEVELS), f32),
            ),
            in_specs=[any_space] * 4,
            out_specs=(any_space, pl.BlockSpec(memory_space=pltpu.VMEM)),
            scratch_shapes=[
                pltpu.VMEM((steps + 1, two, slots, *tile), f32),
                pltpu.VMEM((steps, slots, *tile), i32),
                pltpu.VMEM((steps, slots, *tile), i32),
                pltpu.VMEM((steps, slots // 2, *tile), i32),
                pltpu.VMEM((two, slots, *tile), f32),
                pltpu.VMEM((two, slots, *tile), f32),
                pltpu.VMEM((steps, slots, *tile), i32),
                halo, halo, halo, halo,
                code, code, code,
                edge, edge, edge,
                pltpu.VMEM(tile, f32),
                pltpu.VMEM((ny - 1, *tile), f32),
                pltpu.VMEM(tile, f32),
                pltpu.VMEM((nx, *tile), f32),
                dma((4,)), dma,
                dma((steps, 2, CHUNKS)), dma((steps, CHUNKS)), dma((steps, CHUNKS)),
                dma((2,)), dma, dma,
                dma((steps, 2, CHUNKS)), dma((steps, CHUNKS)), dma((steps, CHUNKS)),
                dma((ny - 1,)), dma((ny - 1,)), dma((nx - 1,)), dma((nx - 1,)),
            ],
            compiler_params=pltpu.CompilerParams(collective_id=0, has_side_effects=True),
        )(view(droplets), view(moves), view(pairing), view(collisions))
        out = out.reshape(two, slots, tiles, cols, LANES).swapaxes(2, 3).reshape(droplets.shape)
        return out, moments

    placed = P(None, None, "gx", "gy")
    return jax.shard_map(
        body, mesh=mesh, in_specs=(placed,) * 4, out_specs=(placed, P()), check_vma=False
    )
```

time: 108 us -> 35.7 us (0.33)
  blocking collectives: 40.4 us -> 0 us
  Pallas kernels: 0 us -> 32.6 us
  other arithmetic: 23.8 us -> 0 us
  local copies, waits for them, and re-layouts: 25.6 us -> 2.25 us
  starting transfers between devices: 13.8 us -> 0 us
  waiting for transfers between devices: 2.67 us -> 0 us
    psum x1 -> x0, blocking collectives: 40.4 us -> none  [shards(): totals.append(lax.psum(terms, ('gx', 'gy')))]
    pallas_call x0 -> x1, Pallas kernels: none -> 32.6 us  [body(): pl.pallas_call(functools.partial(kernel, nx, ny, slots, steps, scale), ou...]
    ppermute x8 -> x0, starting transfers between devices: 13.8 us -> none  [the longest x4 10.7 us: padded(): after = lax.ppermute(leading, axis, down)]
    slice x34 -> x0, local copies, waits for them, and re-layouts: 10.4 us -> none  [the longest x4 3.72 us: padded(): leading = lax.slice_in_dim(array, 0, width, axis=dim)]
    reduce_sum x22 -> x0, other arithmetic: 8.25 us -> none  [the longest x4 1.7 us: pair_column(): counts_p = jnp.sum(jnp.where(hits, counts[None], 0), axis=1)]
    ppermute x4 -> x0, local copies, waits for them, and re-layouts: 6.17 us -> none  [the longest x2 3.87 us: padded(): before = lax.ppermute(last, axis, up)]
    another operation x21 -> x0, other arithmetic: 4.19 us -> none  [the longest x6 1.54 us: pair_column(): jnp.stack([first_new, second_new], axis=1).reshape(counts_p.shape)]
    eq x2 -> x0, other arithmetic: 3.36 us -> none  [spread(): chosen = jnp.where((codes == direction)[None], state, jnp.zeros_like(state))]
  transfers between devices with their start and end apart: 8 -> 0, of which waited for: 5 -> 0; matrix products, arithmetic and copies ran while one was open for 20% -> 0% of each run, Pallas kernels for 0% -> 0%
where the time goes in v1:
time: 35.7 us; the launch traced here: 35.5 us
  Pallas kernels  32.6 us (91%)
  local copies, waits for them, and re-layouts  2.25 us (6%)
  between operations  0.65 us (2%)
    pallas_call x1, Pallas kernels, body(): pl.pallas_call(functools.partial(kernel, nx, ny, slots, steps, scale), ou...  32.6 us
    unnamed x4, local copies, waits for them, and re-layouts  2.25 us

profile of v1, /device:TPU:0, one launch (start us, length us, event | category | flops | bytes accessed | tf_op | source)
XLA Modules:
  0.0 35.5 jit_solution(9135384611731134424)
XLA Ops:
  0.6 32.6 %shard_map.59 = (f32[2,32,8,128]{3,2,1,0:T(8,128)}, f32[2,2,16]{2,1,0:T(2,128)}) custom-call(f32[2,32,8,128]{3,2,1,0:T(8,128)} %bitcast.25, s32[2,32,8,128]{3,2,1,0:T(8,128)} %bitcast.26, s32[2,32,8,128]{3,2,1,0:T(8,128)} %bitcast.27, s32[2,16,8,128]{3,2,1,0:T(8,128)} %bitcast.29), custom_call_target="tpu_custom_call" | custom-call | tf_op jit(solution)/shard_map/pallas_call | solution.py:342
  33.3 0.0 copy-start
  33.3 1.7 %copy.13 = f32[2,32,2,512]{3,2,1,0:T(2,128)} copy(f32[2,32,2,512]{3,2,1,0:T(2,128)} %bitcast.28) | data formatting | bytes 524288
  34.9 0.0 copy-done
  34.9 0.6 %copy.14 = f32[2,2,16]{2,1,0:T(2,128)} copy(f32[2,2,16]{2,1,0:T(2,128)S(1)} %copy-done) | data formatting | bytes 512
Async XLA Ops:
  33.3 1.7 %copy-start = (f32[2,2,16]{2,1,0:T(2,128)S(1)}, f32[2,2,16]{2,1,0:T(2,128)}, u32[]{:S(2)}) copy-start(f32[2,2,16]{2,1,0:T(2,128)} %get-tuple-element.9) | copy-start | bytes 772

commit v2 on v1

v2 whole, which is shorter than its diff:
```python
import functools

import jax
import jax.numpy as jnp
from jax import lax
from jax.experimental import pallas as pl
from jax.experimental.pallas import tpu as pltpu
from jax.sharding import PartitionSpec as P

LEVELS = 16
LANES = 128
ROWS = 8
CHUNKS = 4
count_unit = 4096.0
MESH = pl.DeviceIdType.MESH


def roll(value, shift, axis):
    shift = shift % value.shape[axis]
    return value if shift == 0 else pltpu.roll(value, shift, axis)


def tree(values, bits):
    level = 0
    while len(values) > 1:
        values = [
            jnp.where(bits[level], values[i + 1], values[i]) for i in range(0, len(values), 2)
        ]
        level += 1
    return values[0]


def collide(na, nb, ma, mb, tries):
    first = na >= nb
    big, small = jnp.maximum(na, nb), jnp.minimum(na, nb)
    big_m, small_m = jnp.where(first, ma, mb), jnp.where(first, mb, ma)
    most = jnp.where(3.0 * small <= big, 3.0, jnp.where(2.0 * small <= big, 2.0, 1.0))
    taken = jnp.minimum(tries.astype(jnp.float32), most)
    remain = big - taken * small
    split = remain == 0.0
    half = jnp.floor(small * 0.5)
    big_new = jnp.where(split, half, remain)
    small_new = jnp.where(split, small - half, small)
    grown = small_m + taken * big_m
    big_m_new = jnp.where(split, grown, big_m)
    return (
        jnp.where(first, big_new, small_new),
        jnp.where(first, small_new, big_new),
        jnp.where(first, big_m_new, grown),
        jnp.where(first, grown, big_m_new),
    )


def kernel(
    nx, ny, slots, steps, scale,
    drops_hbm, moves_hbm, order_hbm, tries_hbm, out_ref, mom_ref,
    cur, moves, order, tries, moved, paired, cy_ref,
    send_l, send_r, halo_l, halo_r,
    code_send, code_l, code_r,
    rim, rim_l, rim_r, rim_code, edge_send, edge_dn, edge_up,
    in_sem, xs_sem, xl_sem, xr_sem, cs_sem, cl_sem, cr_sem,
    rs_sem, rl_sem, rr_sem, es_sem, ed_sem, eu_sem, *sums_refs,
):
    gx, gy = lax.axis_index("gx"), lax.axis_index("gy")
    left, right = (lax.rem(gx + nx - 1, nx), gy), (lax.rem(gx + 1, nx), gy)
    down, up = (gx, lax.rem(gy + ny - 1, ny)), (gx, lax.rem(gy + 1, ny))
    width = slots // CHUNKS
    per = width // 2
    stages = sum_stages(nx, ny, gx, gy)

    barrier = pltpu.get_barrier_semaphore()
    greeted = 0
    for size, me, device in stages:
        for d in range(1, size):
            pl.semaphore_signal(barrier, inc=1, device_id=device(lax.rem(me + d, size)), device_id_type=MESH)
        greeted += size - 1

    loads = [
        pltpu.make_async_copy(src, dst, in_sem.at[i])
        for i, (src, dst) in enumerate(
            [(drops_hbm, cur.at[0]), (moves_hbm, moves), (order_hbm, order), (tries_hbm, tries)]
        )
    ]
    for load in loads:
        load.start()

    row = lax.broadcasted_iota(jnp.int32, (ROWS, LANES), 0)
    lane = lax.broadcasted_iota(jnp.int32, (ROWS, LANES), 1)
    even = lax.rem(row, 2) == 0
    group = lane // LEVELS
    groups = LANES // LEVELS

    def remote(src, dst, ss, rs, dev):
        return pltpu.make_async_remote_copy(
            src_ref=src, dst_ref=dst, send_sem=ss, recv_sem=rs, device_id=dev, device_id_type=MESH
        )

    def x_copies(step, q):
        return [
            remote(send_r.at[step, q], halo_l.at[step, q], xs_sem.at[step, 0, q], xl_sem.at[step, q], right),
            remote(send_l.at[step, q], halo_r.at[step, q], xs_sem.at[step, 1, q], xr_sem.at[step, q], left),
        ]

    def rim_copies(step):
        return [
            remote(rim.at[step, 1], rim_l.at[step], rs_sem.at[step, 0], rl_sem.at[step], right),
            remote(rim.at[step, 0], rim_r.at[step], rs_sem.at[step, 1], rr_sem.at[step], left),
        ]

    def start(copies):
        for c in copies:
            c.start()

    def wait(copies):
        for c in copies:
            c.wait()

    def pack_sides(step, q, v, values):
        for t in range(per):
            a, b = values[t], values[per + t]
            send_r[step, q, v, t] = jnp.where(even, roll(a, -1, 0), b)
            send_l[step, q, v, t] = jnp.where(even, a, roll(b, 1, 0))

    def pack_rim(values):
        packed = jnp.zeros((ROWS, LANES), values[0].dtype)
        for g, value in enumerate(values):
            ends = jnp.where(row < 2, value, roll(value, LEVELS, 1))
            packed = jnp.where(group == g, roll(ends, LEVELS * g, 1), packed)
        return packed

    def store_rim(step, q, v, values):
        packed = pack_rim(values)
        for c in range(2):
            rim[step, c, v, pl.ds(2 * q, 1), :] = packed[c : c + 1]
            rim[step, c, v, pl.ds(2 * q + 1, 1), :] = packed[ROWS - 2 + c : ROWS - 1 + c]

    loads[1].wait()
    for step in range(steps):
        packed = jnp.zeros((ROWS, LANES), jnp.int32)
        for q in range(CHUNKS):
            part = pack_rim([moves[step, q * width + g] for g in range(width)])
            packed = jnp.where(row // 2 == q, roll(part, 2 * q, 0), packed)
            rim_code[step, 2 * q : 2 * q + 1, :] = part[0:1]
            rim_code[step, 2 * q + 1 : 2 * q + 2, :] = part[ROWS - 2 : ROWS - 1]
        code_send[step] = packed
    loads[0].wait()
    for q in range(CHUNKS):
        for v in range(2):
            values = [cur[0, v, q * width + g] for g in range(width)]
            store_rim(0, q, v, values)
            pack_sides(0, q, v, values)
    pl.semaphore_wait(barrier, greeted)
    code_copies = [
        remote(code_send, code_l, cs_sem.at[0], cl_sem, right),
        remote(code_send, code_r, cs_sem.at[1], cr_sem, left),
    ]
    start(rim_copies(0))
    start(code_copies)
    for q in range(CHUNKS):
        start(x_copies(0, q))

    def edge_copies(step):
        out = [remote(edge_send.at[step], edge_dn.at[step], es_sem.at[step, 0], ed_sem.at[step], up)]
        if ny > 2:
            out.append(remote(edge_send.at[step], edge_up.at[step], es_sem.at[step, 1], eu_sem.at[step], down))
        return out

    def send_edges(step):
        wait(rim_copies(step))
        code = rim_code[step]
        for v in range(2):
            first, last = rim[step, 0, v], rim[step, 1, v]
            before, after = rim_l[step, v], rim_r[step, v]
            stay, ahead = (code >= 3) & (code < 6), code >= 6
            edge_send[step, 0, v] = jnp.where(stay, first, jnp.where(ahead, before, last))
            edge_send[step, 1, v] = jnp.where(stay, last, jnp.where(ahead, first, after))
        start(edge_copies(step))

    send_edges(0)
    wait(code_copies)
    for step in range(steps):
        own = code_send[step]
        swapped = jnp.where(even, roll(own, -1, 0), roll(own, 1, 0))
        outer = jnp.where(even, roll(code_l[step], -1, 0), roll(code_r[step], 1, 0))
        from_halo = jnp.where(even, own, 8 - own) >= 6
        landed = jnp.where((own >= 3) & (own < 6), own, jnp.where(from_halo, outer, swapped))
        y_step = lax.rem(landed, 3) - 1
        for q in range(CHUNKS):
            lift = roll(y_step, -2 * q, 0)
            lift = jnp.where(row < 2, lift, 0)
            lift = lift + roll(lift, 2, 0)
            lift = lift + roll(lift, 4, 0)
            for g in range(width):
                one = jnp.where(group == 0, roll(lift, -LEVELS * g, 1), 0)
                span = LEVELS
                while span < LANES:
                    one = one + roll(one, span, 1)
                    span *= 2
                cy_ref[step, q * width + g] = one

    row_totals = []
    for step in range(steps):
        if step:
            send_edges(step)
        wait(edge_copies(step))
        above = edge_up if ny > 2 else edge_dn
        for q in range(CHUNKS):
            wait(x_copies(step, q))
            for v in range(2):
                low = jnp.where(
                    even, edge_dn[step, 0, v, 2 * q + 1 : 2 * q + 2, :], edge_dn[step, 1, v, 2 * q + 1 : 2 * q + 2, :]
                )
                high = jnp.where(
                    even, above[step, 0, v, 2 * q : 2 * q + 1, :], above[step, 1, v, 2 * q : 2 * q + 1, :]
                )
                for g in range(width):
                    s, t = q * width + g, g % per
                    hl, hr = halo_l[step, q, v, t], halo_r[step, q, v, t]
                    if g < per:
                        outer = jnp.where(even, hl, roll(hr, 1, 0))
                    else:
                        outer = jnp.where(even, roll(hl, -1, 0), hr)
                    mine, code = cur[step, v, s], moves[step, s]
                    swapped = jnp.where(even, roll(mine, -1, 0), roll(mine, 1, 0))
                    from_halo = jnp.where(even, code, 8 - code) >= 6
                    mine = jnp.where(
                        (code >= 3) & (code < 6), mine, jnp.where(from_halo, outer, swapped)
                    )
                    dy = cy_ref[step, s]
                    fwd, bwd = roll(mine, LEVELS, 1), roll(mine, -LEVELS, 1)
                    fwd_in = jnp.where(row < 2, roll(low, -LEVELS * g, 1), roll(fwd, 2, 0))
                    bwd_in = jnp.where(row >= ROWS - 2, roll(high, -LEVELS * (g + 1), 1), roll(bwd, -2, 0))
                    fwd = jnp.where(group == 0, fwd_in, fwd)
                    bwd = jnp.where(group == groups - 1, bwd_in, bwd)
                    moved[v, s] = jnp.where(dy == 0, mine, jnp.where(dy > 0, fwd, bwd))
        if step == 0:
            wait(loads[2:])

        def pair_body(i, _):
            found = []
            for k in range(2):
                index = order[step, 2 * i + k]
                bits = [(index & (1 << b)) != 0 for b in range((slots - 1).bit_length())]
                for v in range(2):
                    found.append(tree([moved[v, s] for s in range(slots)], bits))
            na, ma, nb, mb = found
            na, nb, ma, mb = collide(na, nb, ma, mb, tries[step, i])
            paired[0, 2 * i] = na
            paired[0, 2 * i + 1] = nb
            paired[1, 2 * i] = ma
            paired[1, 2 * i + 1] = mb
            return 0

        lax.fori_loop(0, slots // 2, pair_body, 0)

        def slot_body(q, sums):
            base = q * width
            counts = [jnp.zeros((ROWS, LANES), jnp.float32)] * width
            masses = [jnp.zeros((ROWS, LANES), jnp.float32)] * width
            for p in range(slots):
                index = order[step, p] - base
                pn, pm = paired[0, p], paired[1, p]
                for k in range(width):
                    hit = index == k
                    counts[k] = jnp.where(hit, pn, counts[k])
                    masses[k] = jnp.where(hit, pm, masses[k])
            if step + 1 < steps:
                pack_sides(step + 1, q, 0, counts)
                pack_sides(step + 1, q, 1, masses)
            count, liquid = sums
            target = cur.at[step + 1] if step + 1 < steps else out_ref
            for k in range(width):
                target[0, base + k] = counts[k]
                target[1, base + k] = masses[k]
                count = count + counts[k]
                liquid = liquid + counts[k] * masses[k]
            if step + 1 < steps:
                store_rim(step + 1, q, 0, counts)
                store_rim(step + 1, q, 1, masses)
                start(x_copies(step + 1, q))
            return count, liquid

        zero = jnp.zeros((ROWS, LANES), jnp.float32)
        sums = lax.fori_loop(0, CHUNKS, slot_body, (zero, zero))
        if step + 1 < steps:
            start(rim_copies(step + 1))
        for total in sums:
            shift = ROWS // 2
            while shift:
                total = total + roll(total, shift, 0)
                shift //= 2
            shift = LANES // 2
            while shift >= LEVELS:
                total = total + roll(total, shift, 1)
                shift //= 2
            row_totals.append(total)

    total = row_totals[0]
    for i in range(1, len(row_totals)):
        total = jnp.where(group == i, row_totals[i], total)
    total = total[0:1]
    for k, (size, me, device) in enumerate(stages):
        part, got, ss, rs = sums_refs[4 * k : 4 * k + 4]
        part[...] = total
        got[me] = total
        sends = [
            remote(part, got.at[me], ss.at[d - 1], rs.at[d - 1], device(lax.rem(me + d, size)))
            for d in range(1, size)
        ]
        start(sends)
        wait(sends)
        terms = [got[i] for i in range(size)]
        while len(terms) > 1:
            terms = [sum(terms[i + 1 : i + 2], terms[i]) for i in range(0, len(terms), 2)]
        total = terms[0]
    total = jnp.broadcast_to(total * scale, (ROWS, LANES))
    for i in range(steps):
        for v in range(2):
            mom_ref[i, v : v + 1, :] = roll(total, -LEVELS * (2 * i + v), 1)[0:1, :LEVELS]


def sum_stages(nx, ny, gx, gy):
    if nx * ny <= 64:
        return [(nx * ny, gx * ny + gy, lambda p: (p // ny, lax.rem(p, ny)))]
    return [(ny, gy, lambda p: (gx, p)), (nx, gx, lambda p: (p, gy))]


def solution(mesh):
    nx, ny = mesh.shape["gx"], mesh.shape["gy"]

    def body(droplets, moves, pairing, collisions):
        two, slots, cols, flat = droplets.shape
        steps, tiles = moves.shape[0], flat // LANES
        assert cols * tiles == ROWS and cols == 2

        def view(a):
            lead = a.shape[:2]
            return a.reshape(*lead, cols, tiles, LANES).swapaxes(2, 3).reshape(*lead, ROWS, LANES)

        f32, i32 = jnp.float32, jnp.int32
        tile = (ROWS, LANES)
        per = slots // 2 // CHUNKS
        dma = pltpu.SemaphoreType.DMA
        halo = pltpu.VMEM((steps, CHUNKS, 2, per, *tile), f32)
        edge = pltpu.VMEM((steps, 2, 2, *tile), f32)
        rim = pltpu.VMEM((steps, 2, *tile), f32)
        sums = []
        for size, _, _ in sum_stages(nx, ny, 0, 0):
            sums += [pltpu.VMEM((1, LANES), f32), pltpu.VMEM((size, 1, LANES), f32), dma((size - 1,)), dma((size - 1,))]
        code = pltpu.VMEM((steps, *tile), i32)
        scale = 1.0 / (cols * nx * (flat // LEVELS) * ny * count_unit)
        any_space = pl.BlockSpec(memory_space=pl.ANY)
        out, moments = pl.pallas_call(
            functools.partial(kernel, nx, ny, slots, steps, scale),
            out_shape=(
                pltpu.VMEM((two, slots, *tile), f32),
                jax.ShapeDtypeStruct((steps, 2, LEVELS), f32),
            ),
            in_specs=[any_space] * 4,
            out_specs=(pl.BlockSpec(memory_space=pltpu.VMEM), pl.BlockSpec(memory_space=pltpu.VMEM)),
            scratch_shapes=[
                pltpu.VMEM((steps, two, slots, *tile), f32),
                pltpu.VMEM((steps, slots, *tile), i32),
                pltpu.VMEM((steps, slots, *tile), i32),
                pltpu.VMEM((steps, slots // 2, *tile), i32),
                pltpu.VMEM((two, slots, *tile), f32),
                pltpu.VMEM((two, slots, *tile), f32),
                pltpu.VMEM((steps, slots, *tile), i32),
                halo, halo, halo, halo,
                code, code, code,
                edge, rim, rim, code, edge, edge, edge,
                dma((4,)),
                dma((steps, 2, CHUNKS)), dma((steps, CHUNKS)), dma((steps, CHUNKS)),
                dma((2,)), dma, dma,
                dma((steps, 2)), dma((steps,)), dma((steps,)),
                dma((steps, 2)), dma((steps,)), dma((steps,)),
                *sums,
            ],
            compiler_params=pltpu.CompilerParams(collective_id=0, has_side_effects=True),
        )(view(droplets), view(moves), view(pairing), view(collisions))
        out = out.reshape(two, slots, tiles, cols, LANES).swapaxes(2, 3).reshape(droplets.shape)
        return out, moments

    placed = P(None, None, "gx", "gy")
    return jax.shard_map(
        body, mesh=mesh, in_specs=(placed,) * 4, out_specs=(placed, P()), check_vma=False
    )
```

time: 35.7 us -> 33.6 us (0.941)
  Pallas kernels: 32.6 us -> 31.5 us
  local copies, waits for them, and re-layouts: 2.25 us -> 1.29 us
    pallas_call x1, Pallas kernels: 32.6 us -> 31.5 us  [body(): pl.pallas_call(functools.partial(kernel, nx, ny, slots, steps, scale), ou...]
    unnamed x4, local copies, waits for them, and re-layouts: 2.25 us -> 1.29 us
where the time goes in v2:
time: 33.6 us; the launch traced here: 33.5 us
  Pallas kernels  31.5 us (94%)
  local copies, waits for them, and re-layouts  1.29 us (4%)
  between operations  0.65 us (2%)
    pallas_call x1, Pallas kernels, body(): pl.pallas_call(functools.partial(kernel, nx, ny, slots, steps, scale), ou...  31.5 us
    unnamed x4, local copies, waits for them, and re-layouts  1.29 us

profile of v2, /device:TPU:0, one launch (start us, length us, event | category | flops | bytes accessed | tf_op | source)
XLA Modules:
  0.0 33.5 jit_solution(18228402096679553592)
XLA Ops:
  0.6 31.5 %shard_map.59 = (f32[2,32,8,128]{3,2,1,0:T(8,128)S(1)}, f32[2,2,16]{2,1,0:T(2,128)}) custom-call(f32[2,32,8,128]{3,2,1,0:T(8,128)} %bitcast.26, s32[2,32,8,128]{3,2,1,0:T(8,128)} %bitcast.27, s32[2,32,8,128]{3,2,1,0:T(8,128)} %bitcast.28, s32[2,16,8,128]{3,2,1,0:T(8,128)} %bitcast.29), custom_call_target="tpu_custom_call" | custom-call | tf_op jit(solution)/shard_map/pallas_call | solution.py:353
  32.2 0.0 copy-start
  32.2 0.7 %copy.13 = f32[2,32,2,512]{3,2,1,0:T(2,128)} copy(f32[2,32,2,512]{3,2,1,0:T(2,128)S(1)} %bitcast.25) | data formatting | bytes 524288
  32.9 0.0 copy-done
  32.9 0.6 %copy.14 = f32[2,2,16]{2,1,0:T(2,128)} copy(f32[2,2,16]{2,1,0:T(2,128)S(1)} %copy-done) | data formatting | bytes 512
Async XLA Ops:
  32.2 0.7 %copy-start = (f32[2,2,16]{2,1,0:T(2,128)S(1)}, f32[2,2,16]{2,1,0:T(2,128)}, u32[]{:S(2)}) copy-start(f32[2,2,16]{2,1,0:T(2,128)} %get-tuple-element.11) | copy-start | bytes 772

commit v3 on v2

--- a/solution.py
+++ b/solution.py
@@ -277,13 +277,15 @@
             if step + 1 < steps:
                 store_rim(step + 1, q, 0, counts)
                 store_rim(step + 1, q, 1, masses)
-                start(x_copies(step + 1, q))
+                pl.when(q == 0)(lambda: start(x_copies(step + 1, 0)))
             return count, liquid
 
         zero = jnp.zeros((ROWS, LANES), jnp.float32)
         sums = lax.fori_loop(0, CHUNKS, slot_body, (zero, zero))
         if step + 1 < steps:
             start(rim_copies(step + 1))
+            for q in range(1, CHUNKS):
+                start(x_copies(step + 1, q))
         for total in sums:
             shift = ROWS // 2
             while shift:

time: 33.6 us -> 32.5 us (0.967)
  Pallas kernels: 31.5 us -> 30.4 us
    pallas_call x1, Pallas kernels: 31.5 us -> 30.4 us  [body(): pl.pallas_call(functools.partial(kernel, nx, ny, slots, steps, scale), ou...]
where the time goes in v3:
time: 32.5 us; the launch traced here: 32.3 us
  Pallas kernels  30.4 us (94%)
  local copies, waits for them, and re-layouts  1.29 us (4%)
  between operations  0.65 us (2%)
    pallas_call x1, Pallas kernels, body(): pl.pallas_call(functools.partial(kernel, nx, ny, slots, steps, scale), ou...  30.4 us
    unnamed x4, local copies, waits for them, and re-layouts  1.29 us

profile of v3, /device:TPU:0, one launch (start us, length us, event | category | flops | bytes accessed | tf_op | source)
XLA Modules:
  0.0 32.3 jit_solution(14624607231335258393)
XLA Ops:
  0.6 30.4 %shard_map.59 = (f32[2,32,8,128]{3,2,1,0:T(8,128)S(1)}, f32[2,2,16]{2,1,0:T(2,128)}) custom-call(f32[2,32,8,128]{3,2,1,0:T(8,128)} %bitcast.26, s32[2,32,8,128]{3,2,1,0:T(8,128)} %bitcast.27, s32[2,32,8,128]{3,2,1,0:T(8,128)} %bitcast.28, s32[2,16,8,128]{3,2,1,0:T(8,128)} %bitcast.29), custom_call_target="tpu_custom_call" | custom-call | tf_op jit(solution)/shard_map/pallas_call | solution.py:355
  31.0 0.0 copy-start
  31.0 0.7 %copy.13 = f32[2,32,2,512]{3,2,1,0:T(2,128)} copy(f32[2,32,2,512]{3,2,1,0:T(2,128)S(1)} %bitcast.25) | data formatting | bytes 524288
  31.7 0.0 copy-done
  31.7 0.6 %copy.14 = f32[2,2,16]{2,1,0:T(2,128)} copy(f32[2,2,16]{2,1,0:T(2,128)S(1)} %copy-done) | data formatting | bytes 512
Async XLA Ops:
  31.0 0.7 %copy-start = (f32[2,2,16]{2,1,0:T(2,128)S(1)}, f32[2,2,16]{2,1,0:T(2,128)}, u32[]{:S(2)}) copy-start(f32[2,2,16]{2,1,0:T(2,128)} %get-tuple-element.11) | copy-start | bytes 772
